TPU v7x, 32 devices: a whole 2x2x4 slice. The times are simulated.
32 devices in a mesh: blk: 8 (over y, x, core), uly: 1, dp: 4 (over z).
Axes of the slice: x: 2, y: 2, z: 4, core: 2. Of those that a mesh axis runs over, the one named last changes fastest.
Arguments:
- short_tokens: bfloat16 [32, 1024, 4096], P(('blk', 'dp'), 'uly'), may hold values from -150 to 150, as said below
- short_segments: int32 [32, 1024], P(('blk', 'dp')), may hold values from 0 to 3, never falling along the last dimension, each value on 1 to 512 neighbouring positions
- long_tokens: bfloat16 [4, 3072, 4096], P('dp', 'blk'), may hold values from -150 to 150, as said below
- long_lengths: int32 [4], P('dp'), may hold values from 768 to 3072
- w_query: bfloat16 [4096, 2048], P(('blk', 'dp'), 'uly'), may hold values from -0.09375 to 0.09375
- w_key: bfloat16 [4096, 512], P(('blk', 'dp'), 'uly'), may hold values from -0.09375 to 0.09375
- w_value: bfloat16 [4096, 512], P(('blk', 'dp'), 'uly'), may hold values from -0.09375 to 0.09375
Outputs:
- short_out: bfloat16 [32, 1024, 2048], P(('blk', 'dp'), 'uly')
- long_out: bfloat16 [4, 3072, 2048], P('dp', 'blk', 'uly')
Inputs may be any that keep to these rules, and one draw needn't show every extreme that they name: `short_tokens`: activations of the short bucket. `long_tokens`: activations of the long bucket; rows at or after a sequence's length are padding. `short_segments`: document numbers never fall along a sequence. `long_lengths`: a long sequence occupies positions 0 to its length - 1 of its 3072 slots.
All inputs are finite; a program needn't handle non-finite values.
Results may differ from a plain program's by a relative error of at most 0.012.
The roundings to bfloat16 on the way count: a program that leaves them out, or rounds other values in their place, can miss the bound.
Values may be sent and summed in bfloat16 or wider, within the bound.
A program may use at most 128 MiB of HBM per device.

v0:
```python
import math
import jax
import jax.numpy as jnp
from jax import lax
from jax.sharding import PartitionSpec as P

HD = 128
masked_score = -1e30


def head_scores(query_rows, key_rows, kv_heads):
    query_heads = query_rows.reshape(query_rows.shape[0], kv_heads, -1, HD)
    key_heads = key_rows.reshape(key_rows.shape[0], kv_heads, HD)
    scores = jnp.einsum(
        "bhgd,khd->hgbk", query_heads, key_heads, preferred_element_type=jnp.float32
    )
    return scores * (1.0 / math.sqrt(HD))


def weighted_values(probabilities, value_rows, kv_heads):
    value_heads = value_rows.reshape(value_rows.shape[0], kv_heads, HD)
    return jnp.einsum(
        "hgbk,khd->hgbd", probabilities, value_heads, preferred_element_type=jnp.float32
    )


def short_attention(queries, key_rows, value_rows, segments):
    kv_heads = key_rows.shape[1] // HD
    seq_len = key_rows.shape[0]
    block_rows = min(512, seq_len)
    positions = jnp.arange(seq_len, dtype=jnp.int32)
    outputs = []
    for block_index in range(seq_len // block_rows):
        first_row = block_index * block_rows
        query_pos = positions[first_row : first_row + block_rows]
        query_seg = segments[first_row : first_row + block_rows]
        visible = (positions[None, :] <= query_pos[:, None]) & (
            segments[None, :] == query_seg[:, None]
        )
        scores = head_scores(queries[first_row : first_row + block_rows], key_rows, kv_heads)
        scores = jnp.where(visible, scores, masked_score)
        row_max = jnp.max(scores, axis=-1, keepdims=True)
        exponentials = jnp.where(visible, jnp.exp(scores - row_max), 0.0)
        totals = jnp.sum(exponentials, axis=-1)
        mixed = (
            weighted_values(exponentials.astype(jnp.bfloat16), value_rows, kv_heads)
            / totals[..., None]
        )
        outputs.append(jnp.transpose(mixed, (2, 0, 1, 3)).reshape(block_rows, -1))
    return jnp.concatenate(outputs, axis=0).astype(jnp.bfloat16)


def local(short_tokens, short_segments, long_tokens, long_lengths, w_query, w_key, w_value):
    short_rows = short_tokens[0]
    long_rows = long_tokens[0]
    long_count = long_rows.shape[0]
    query_cols = w_query.shape[1]
    kv_cols = w_key.shape[1]
    whole_rows = lax.all_gather(short_rows, "uly", axis=0, tiled=True)
    pieces = (
        lax.all_gather(w_query, ("blk", "dp"), axis=0, tiled=True),
        lax.all_gather(w_key, ("blk", "dp"), axis=0, tiled=True),
        lax.all_gather(w_value, ("blk", "dp"), axis=0, tiled=True),
    )
    short_new = tuple(
        (jnp.dot(whole_rows, pieces[i], preferred_element_type=jnp.float32) for i in range(3))
    )
    long_new = tuple(
        (jnp.dot(long_rows, pieces[i], preferred_element_type=jnp.float32) for i in range(3))
    )
    projected = short_new + long_new
    query_short, key_short, value_short = tuple(
        (item.astype(jnp.bfloat16) for item in projected[:3])
    )
    query_long, key_long, value_long = tuple((item.astype(jnp.bfloat16) for item in projected[3:]))
    attended = short_attention(query_short, key_short, value_short, short_segments[0])
    short_back = lax.all_to_all(attended, "uly", split_axis=0, concat_axis=1, tiled=True)
    long_len = long_lengths[0]
    query_pos = lax.axis_index("blk") * long_count + jnp.arange(long_count, dtype=jnp.int32)
    kv_heads = kv_cols // HD
    group_size = query_cols // kv_cols
    cycle_init = (
        jnp.full((kv_heads, group_size, long_count), masked_score, jnp.float32),
        jnp.zeros((kv_heads, group_size, long_count), jnp.float32),
        jnp.zeros((kv_heads, group_size, long_count, HD), jnp.float32),
    )
    carry = cycle_init
    key_piece = lax.all_gather(key_long, "blk", axis=0, tiled=True)
    value_piece = lax.all_gather(value_long, "blk", axis=0, tiled=True)
    piece_rows = key_piece.shape[0]
    block_rows = math.gcd(piece_rows, 512)
    blocks_count = piece_rows // block_rows
    key_blocks = key_piece.reshape(blocks_count, block_rows, -1)
    value_blocks = value_piece.reshape(blocks_count, block_rows, -1)
    block_starts = block_rows * jnp.arange(blocks_count, dtype=jnp.int32)

    def update(states, block_key, block_value, block_start):
        running_max, running_sum, accumulated = states
        key_pos = block_start + jnp.arange(block_rows, dtype=jnp.int32)
        visible = (key_pos[None, :] <= query_pos[:, None]) & (key_pos[None, :] < long_len)
        scores = jnp.where(visible, head_scores(query_long, block_key, kv_heads), masked_score)
        new_max = jnp.maximum(running_max, jnp.max(scores, axis=-1))
        rescale = jnp.exp(running_max - new_max)
        exponentials = jnp.where(visible, jnp.exp(scores - new_max[..., None]), 0.0)
        running_sum = running_sum * rescale + jnp.sum(exponentials, axis=-1)
        accumulated = accumulated * rescale[..., None] + weighted_values(
            exponentials.astype(jnp.bfloat16), block_value, kv_heads
        )
        return (new_max, running_sum, accumulated)

    def advance(states, inputs):
        block_key, block_value, block_start = inputs
        states = update(states, block_key, block_value, block_start)
        return (states, None)

    carry, unused = lax.scan(advance, carry, (key_blocks, value_blocks, block_starts))
    running_max, running_sum, accumulated = carry
    mixed = accumulated / running_sum[..., None]
    mixed = jnp.transpose(mixed, (2, 0, 1, 3)).reshape(long_count, query_cols)
    mixed = jnp.where(query_pos[:, None] < long_len, mixed, 0.0)
    return (short_back[None], mixed.astype(jnp.bfloat16)[None])


def solution(mesh):
    return jax.shard_map(
        local,
        mesh=mesh,
        in_specs=(
            P(("blk", "dp"), "uly", None),
            P(("blk", "dp"), None),
            P("dp", "blk", None),
            P("dp"),
            P(("blk", "dp"), "uly"),
            P(("blk", "dp"), "uly"),
            P(("blk", "dp"), "uly"),
        ),
        out_specs=(P(("blk", "dp"), "uly", None), P("dp", "blk", "uly")),
        check_vma=False,
    )
```

profile of v0, /device:TPU:0, one launch (start us, length us, event | category | flops | bytes accessed | tf_op | source)
XLA Modules:
  0.0 508.8 jit_solution(50371150435943423)
XLA Ops:
  9.5 65.9 %all-gather.10.cloned.1.call-done = bf16[4096,512]{1,0:T(8,128)(2,1)} async-done(((bf16[128,512]{1,0:T(8,128)(2,1)}), bf16[4096,512]{1,0:T(8,128)(2,1)}) %all-gather.10.cloned.1.call-update) | async-done | bytes 4194320 | tf_op jit(solution)/shard_map/all_gather | solution.py:63
  75.4 4.7 fusion.84
  81.4 1.9 fusion.59
  83.3 55.5 %all-gather.6.cloned.1.call-done = bf16[4096,512]{1,0:T(8,128)(2,1)} async-done(((bf16[128,512]{1,0:T(8,128)(2,1)}), bf16[4096,512]{1,0:T(8,128)(2,1)}) %all-gather.6.cloned.1.call-update) | async-done | bytes 4194320 | tf_op jit(solution)/shard_map/all_gather | solution.py:62
  138.8 4.7 fusion.81
  143.6 10.3 %fusion.78 = bf16[1024,512]{0,1:T(8,128)(2,1)} fusion(bf16[4096,512]{1,0:T(8,128)(2,1)} %all-gather.10.cloned.1.call-done, bf16[1,1024,4096]{2,1,0:T(8,128)(2,1)} %param.9), kind=kOutput, calls=%fused_computation.77 | convolution fusion | flops 4295491584 | bytes 13631488 | tf_op jit(solution)/shard_map/dot_general | solution.py:66
  153.8 8.4 %fusion.75 = bf16[1024,512]{0,1:T(8,128)(2,1)} fusion(bf16[4096,512]{1,0:T(8,128)(2,1)S(1)} %copy-done.10, bf16[1,1024,4096]{2,1,0:T(8,128)(2,1)} %param.9), kind=kOutput, calls=%fused_computation.76 | convolution fusion | flops 4295491584 | bytes 13631488 | tf_op jit(solution)/shard_map/dot_general | solution.py:66
  162.2 92.7 %all-gather.8.cloned.1.call-done = bf16[4096,2048]{1,0:T(8,128)(2,1)} async-done(((bf16[128,2048]{1,0:T(8,128)(2,1)}), bf16[4096,2048]{1,0:T(8,128)(2,1)}) %all-gather.8.cloned.1.call-update) | async-done | bytes 16777232 | tf_op jit(solution)/shard_map/all_gather | solution.py:61
  255.0 22.7 %fusion.43 = bf16[1024,2048]{1,0:T(8,128)(2,1)S(1)} fusion(bf16[4096,2048]{1,0:T(8,128)(2,1)} %all-gather.8.cloned.1.call-done, bf16[1,1024,4096]{2,1,0:T(8,128)(2,1)} %param.9), kind=kOutput, calls=%fused_computation.56 | convolution fusion | flops 17181966336 | bytes 29360128 | tf_op jit(solution)/shard_map/dot_general | solution.py:66
  277.7 2.4 fusion.91
  280.0 4.5 reshape.136
  284.5 11.6 %fusion.52 = bf16[384,2048]{1,0:T(8,128)(2,1)} fusion(bf16[4096,2048]{1,0:T(8,128)(2,1)} %all-gather.8.cloned.1.call-done, bf16[1,384,4096]{2,1,0:T(8,128)(2,1)S(1)} %copy-done), kind=kOutput, calls=%fused_computation.65 | convolution fusion | flops 6443237376 | bytes 21495808 | tf_op jit(solution)/shard_map/dot_general | solution.py:69
  296.1 2.8 reshape.150
  299.0 4.4 reshape.138
  303.4 17.7 %all-gather.12.cloned.1.call-done = bf16[3072,512]{1,0:T(8,128)(2,1)} async-done(((bf16[384,512]{1,0:T(8,128)(2,1)}), bf16[3072,512]{1,0:T(8,128)(2,1)}) %all-gather.12.cloned.1.call-update) | async-done | bytes 3145744 | tf_op jit(solution)/shard_map/all_gather | solution.py:88
  321.1 102.2 %while.16 = (s32[]{:T(128)}, f32[4,4,384]{2,1,0:T(4,128)S(1)}, f32[4,4,384]{2,1,0:T(4,128)S(1)}, f32[4,4,384,128]{3,2,1,0:T(8,128)}, s32[6]{0:T(128)S(1)}, /*ind...) while((s32[]{:T(128)}, f32[4,4,384]{2,1,0:T(4,128)S(1)}, ...), condition=%wide.wide.region_7.8_spmd.clone, body=%wide.wide.region_4.7_spmd.clone.sunk | while | flops 1654292352 | bytes 77209832 | solution.py:116
  325.8 2.7 fusion.136
  328.5 3.0 fusion.137
  331.6 5.1 fusion.139
  342.8 2.7 fusion.136
  345.5 3.0 fusion.137
  348.6 5.1 fusion.139
  353.7 1.6 copy-done.4
  359.8 2.7 fusion.136
  362.5 3.0 fusion.137
  365.6 5.1 fusion.139
  370.7 1.6 copy-done.4
  376.8 2.7 fusion.136
  379.5 3.0 fusion.137
  382.6 5.1 fusion.139
  393.8 2.7 fusion.136
  396.5 3.0 fusion.137
  399.6 5.1 fusion.139
  404.7 1.6 copy-done.4
  410.8 2.7 fusion.136
  413.5 3.0 fusion.137
  416.6 5.1 fusion.139
  421.7 1.6 copy-done.4
  423.4 2.4 divide_bitcast_fusion
  427.0 2.4 reshape.141
  429.4 20.1 %fusion.93 = (f32[4,4,512]{2,1,0:T(4,128)S(1)}, bf16[4,4,512,1024]{2,3,1,0:T(8,128)(2,1)}) fusion(bf16[1024,4,128,1]{0,2,3,1:T(8,128)(2,1)S(1)} %bitcast.156, pred[512,1024]{0,1:T(8,128)(4,1)S(1)} %copy-done.7, bf16[512,4,4,128]{3,2,1,0:T(4,128)(2,1)} %reshape.138), kind=kOutput, calls=%fused_computation.88 | convolution fusion | flops 2197816320 | bytes 20480000 | tf_op jit(solution)/shard_map/sub | solution.py:43
  449.5 9.5 %fusion.41 = bf16[512,4,4,128]{0,3,2,1:T(8,128)(2,1)} fusion(bf16[1024,4,128,1]{0,2,3,1:T(8,128)(2,1)S(1)} %bitcast.154, bf16[4,4,512,1024]{2,3,1,0:T(8,128)(2,1)} %get-tuple-element.136, f32[512,4,4]{0,2,1:T(4,128)S(1)} %bitcast.158), kind=kOutput, calls=%fused_computation.53 | convolution fusion | flops 2149580800 | bytes 19955712 | tf_op jit(solution)/shard_map/hgbk,khd->hgbd/dot_general | solution.py:22
  459.0 4.1 copy.31
  463.1 20.9 %fusion.98 = (f32[4,4,512]{2,1,0:T(4,128)S(1)}, bf16[4,4,512,1024]{2,3,1,0:T(8,128)(2,1)}) fusion(bf16[1024,4,128,1]{0,2,3,1:T(8,128)(2,1)} %bitcast.155, pred[512,1024]{0,1:T(8,128)(4,1)S(1)} %copy-done.6, bf16[512,4,4,128]{3,2,1,0:T(4,128)(2,1)S(1)} %copy-done.5), kind=kOutput, calls=%fused_computation.89 | convolution fusion | flops 2197816320 | bytes 20480000 | tf_op jit(solution)/shard_map/sub | solution.py:43
  484.0 8.5 %fusion.42 = bf16[512,4,4,128]{0,3,2,1:T(8,128)(2,1)S(1)} fusion(bf16[1024,4,128,1]{0,2,3,1:T(8,128)(2,1)} %bitcast.153, bf16[4,4,512,1024]{2,3,1,0:T(8,128)(2,1)} %get-tuple-element.138, f32[512,4,4]{0,2,1:T(4,128)S(1)} %bitcast.157), kind=kOutput, calls=%fused_computation.55 | convolution fusion | flops 2149580800 | bytes 19955712 | tf_op jit(solution)/shard_map/hgbk,khd->hgbd/dot_general | solution.py:22
  492.5 2.4 copy.30
  494.9 3.0 select_convert_fusion
  497.9 4.2 pad_maximum_fusion
  (130 shorter events, 34.4 us)
Async XLA Ops:
  7.2 68.2 %copy-start = (bf16[1,384,4096]{2,1,0:T(8,128)(2,1)S(1)}, bf16[1,384,4096]{2,1,0:T(8,128)(2,1)}, u32[]{:S(2)}) copy-start(bf16[1,384,4096]{2,1,0:T(8,128)(2,1)} %param.11) | copy-start | bytes 9437188
  7.2 68.2 %all-gather.10.cloned.1.call-start = ((), (), s32[]{:S(2)}) async-start(), calls=%async_computation.2 | async-start | bytes 4325376 | tf_op jit(solution)/shard_map/all_gather | solution.py:63
  7.9 130.9 %all-gather.6.cloned.1.call-start = ((), (), s32[]{:S(2)}) async-start(), calls=%async_computation | async-start | bytes 4325376 | tf_op jit(solution)/shard_map/all_gather | solution.py:62
  8.7 246.3 %all-gather.8.cloned.1.call-start = ((), (), s32[]{:S(2)}) async-start(), calls=%async_computation.1 | async-start | bytes 17301504 | tf_op jit(solution)/shard_map/all_gather | solution.py:61
  9.4 72.0 %copy-start.8 = (s32[1,1024]{1,0:T(1,128)S(1)}, s32[1,1024]{1,0:T(1,128)}, u32[]{:S(2)}) copy-start(s32[1,1024]{1,0:T(1,128)} %param.10) | copy-start | bytes 12292
  9.4 294.0 %all-gather.14.cloned.1.call-start = ((), (), s32[]{:S(2)}) async-start(), calls=%async_computation.4 | async-start | bytes 3538944 | tf_op jit(solution)/shard_map/all_gather | solution.py:89
  80.1 241.0 %all-gather.12.cloned.1.call-start = ((), (), s32[]{:S(2)}) async-start(), calls=%async_computation.3 | async-start | bytes 3538944 | tf_op jit(solution)/shard_map/all_gather | solution.py:88
  143.6 10.3 %copy-start.10 = (bf16[4096,512]{1,0:T(8,128)(2,1)S(1)}, bf16[4096,512]{1,0:T(8,128)(2,1)}, u32[]{:S(2)}) copy-start(bf16[4096,512]{1,0:T(8,128)(2,1)} %all-gather.6.cloned.1.call-done) | copy-start | bytes 12582916
  328.5 3.1 copy-start.3
  336.7 1.7 copy-start.4
  345.5 3.1 copy-start.3
  353.7 1.7 copy-start.4
  362.5 3.1 copy-start.3
  370.7 1.7 copy-start.4
  379.5 3.1 copy-start.3
  387.7 1.7 copy-start.4
  396.5 3.1 copy-start.3
  404.7 1.7 copy-start.4
  413.5 3.1 copy-start.3
  421.7 1.7 copy-start.4
  425.8 3.6 copy-start.7
  425.8 3.6 copy-start.12
  429.4 20.1 %copy-start.11 = (bf16[1024,512]{0,1:T(8,128)(2,1)S(1)}, bf16[1024,512]{0,1:T(8,128)(2,1)}, u32[]{:S(2)}) copy-start(bf16[1024,512]{0,1:T(8,128)(2,1)} %fusion.78) | copy-start | bytes 3145732
  459.0 4.1 copy-start.5
  459.0 4.1 copy-start.6
  492.5 2.4 copy-start.9
  494.9 3.0 copy-start.2
  494.9 7.2 %copy-start.1 = (bf16[1,384,4096]{2,1,0:T(8,128)(2,1)S(1)}, bf16[1,384,4096]{2,1,0:T(8,128)(2,1)}, u32[]{:S(2)}) copy-start(bf16[1,384,4096]{2,1,0:T(8,128)(2,1)} %param.11) | copy-start | bytes 9437188
Sparse Core Ops, SparseCore 0:
  11.0 64.3 all-gather.9
  78.4 60.4 all-gather.5
  141.8 113.1 all-gather.7
  256.7 30.3 all-gather.13
  288.9 32.1 all-gather.11
where the time goes:
time: 515 us; the launch traced here: 509 us
  waiting for transfers between devices  234 us (45%)
  matrix products  168 us (33%)
  local copies, waits for them, and re-layouts  48 us (9%)
  other arithmetic  43.3 us (8%)
  between operations  14.8 us (3%)
    all_gather x1, waiting for transfers between devices, local(): lax.all_gather(w_query, ('blk', 'dp'), axis=0, tiled=True)  92.7 us
    all_gather x1, waiting for transfers between devices, local(): lax.all_gather(w_value, ('blk', 'dp'), axis=0, tiled=True)  65.9 us
    all_gather x1, waiting for transfers between devices, local(): lax.all_gather(w_key, ('blk', 'dp'), axis=0, tiled=True)  55.5 us
    dot_general x8, matrix products, weighted_values(): jnp.einsum('hgbk,khd->hgbd', probabilities, value_heads, preferred_elemen...  48.3 us
    dot_general x3, matrix products, local(): jnp.dot(whole_rows, pieces[i], preferred_element_type=jnp.float32)  41.3 us
    sub x2, matrix products, short_attention(): exponentials = jnp.where(visible, jnp.exp(scores - row_max), 0.0)  41 us
    dot_general x3, matrix products, local(): jnp.dot(long_rows, pieces[i], preferred_element_type=jnp.float32)  21.1 us
    reduce_sum x6, other arithmetic, update(): running_sum = running_sum * rescale + jnp.sum(exponentials, axis=-1)  18.2 us
  transfers between devices with their start and end apart: 5, of which 4 were waited for; matrix products, arithmetic and copies ran while one was open for 16% of the time, Pallas kernels for 0%

commit v1 on v0

--- a/solution.py
+++ b/solution.py
@@ -6,6 +6,18 @@
 
 HD = 128
 masked_score = -1e30
+
+
+def doubled_up(x, axis, dim):
+    ways, here, step = (lax.axis_size(axis), lax.axis_index(axis), x.shape[dim])
+    line, have = (x, 1)
+    while have < ways:
+        line = jnp.concatenate(
+            [line, lax.ppermute(line, axis, [(d, (d - have) % ways) for d in range(ways)])],
+            axis=dim,
+        )
+        have = 2 * have
+    return jnp.roll(line, here * step, axis=dim)
 
 
 def head_scores(query_rows, key_rows, kv_heads):
@@ -58,7 +70,7 @@
     kv_cols = w_key.shape[1]
     whole_rows = lax.all_gather(short_rows, "uly", axis=0, tiled=True)
     pieces = (
-        lax.all_gather(w_query, ("blk", "dp"), axis=0, tiled=True),
+        doubled_up(w_query, ("blk", "dp"), 0),
         lax.all_gather(w_key, ("blk", "dp"), axis=0, tiled=True),
         lax.all_gather(w_value, ("blk", "dp"), axis=0, tiled=True),
     )

time: 515 us -> 773 us (1.50)
  waiting for transfers between devices: 234 us -> 366 us
  matrix products: 168 us -> 215 us
  local copies, waits for them, and re-layouts: 48 us -> 83.9 us
  other arithmetic: 43.3 us -> 72.1 us
  starting transfers between devices: 0.19 us -> 12.4 us
    ppermute x0 -> x5, waiting for transfers between devices: none -> 320 us  [doubled_up(): lax.ppermute(line, axis, [(d, (d - have) % ways) for d in range(ways)])]
    all_gather x1 -> x0, waiting for transfers between devices: 92.7 us -> none  [local(): lax.all_gather(w_query, ('blk', 'dp'), axis=0, tiled=True)]
    all_gather x1, waiting for transfers between devices: 55.5 us -> 0.01 us  [local(): lax.all_gather(w_key, ('blk', 'dp'), axis=0, tiled=True)]
    unnamed x22 -> x37, local copies, waits for them, and re-layouts: 0.05 us -> 28.6 us
    dot_general x8, matrix products: 48.3 us -> 71.6 us  [weighted_values(): jnp.einsum('hgbk,khd->hgbd', probabilities, value_heads, preferred_elemen...]
    all_gather x1, waiting for transfers between devices: 65.9 us -> 45.1 us  [local(): lax.all_gather(w_value, ('blk', 'dp'), axis=0, tiled=True)]
    reduce_sum x6, other arithmetic: 18.2 us -> 38.8 us  [update(): running_sum = running_sum * rescale + jnp.sum(exponentials, axis=-1)]
    dot_general x6, matrix products: 16.1 us -> 36 us  [head_scores(): jnp.einsum('bhgd,khd->hgbk', query_heads, key_heads, preferred_element_ty...]
  transfers between devices with their start and end apart: 5 -> 9, of which waited for: 4 -> 6; matrix products, arithmetic and copies ran while one was open for 16% -> 16% of each run, Pallas kernels for 0% -> 0%
where the time goes in v1:
time: 773 us; the launch traced here: 764 us
  waiting for transfers between devices  366 us (47%)
  matrix products  215 us (28%)
  local copies, waits for them, and re-layouts  83.9 us (11%)
  other arithmetic  72.1 us (9%)
  between operations  14.9 us (2%)
  starting transfers between devices  12.4 us (2%)
    ppermute x5, waiting for transfers between devices, doubled_up(): lax.ppermute(line, axis, [(d, (d - have) % ways) for d in range(ways)])  320 us
    dot_general x8, matrix products, weighted_values(): jnp.einsum('hgbk,khd->hgbd', probabilities, value_heads, preferred_elemen...  71.6 us
    all_gather x1, waiting for transfers between devices, local(): lax.all_gather(w_value, ('blk', 'dp'), axis=0, tiled=True)  45.1 us
    dot_general x3, matrix products, local(): jnp.dot(whole_rows, pieces[i], preferred_element_type=jnp.float32)  43.2 us
    sub x2, matrix products, short_attention(): exponentials = jnp.where(visible, jnp.exp(scores - row_max), 0.0)  41.2 us
    reduce_sum x6, other arithmetic, update(): running_sum = running_sum * rescale + jnp.sum(exponentials, axis=-1)  38.8 us
    dot_general x6, matrix products, head_scores(): jnp.einsum('bhgd,khd->hgbk', query_heads, key_heads, preferred_element_ty...  36 us
    unnamed x37, local copies, waits for them, and re-layouts  28.6 us
  transfers between devices with their start and end apart: 9, of which 6 were waited for; matrix products, arithmetic and copies ran while one was open for 16% of the time, Pallas kernels for 0%

profile of v1, /device:TPU:0, one launch (start us, length us, event | category | flops | bytes accessed | tf_op | source)
XLA Modules:
  0.0 764.5 jit_solution(9561387752789478007)
XLA Ops:
  8.0 6.5 collective-permute-start
  14.5 11.6 %collective-permute-done = bf16[128,2048]{1,0:T(8,128)(2,1)} collective-permute-done((bf16[128,2048]{1,0:T(8,128)(2,1)}, bf16[128,2048]{1,0:T(8,128)(2,1)}, u32[]{:S(2)}, u32[]{:S(2)}) %collective-permute-start) | collective-permute-done | bytes 524320 | tf_op jit(solution)/shard_map/ppermute | solution.py:16
  27.9 52.9 %collective-permute-done.1 = bf16[256,2048]{1,0:T(8,128)(2,1)S(1)} collective-permute-done((bf16[256,2048]{1,0:T(8,128)(2,1)S(1)}, bf16[256,2048]{1,0:T(8,128)(2,1)S(1)}, u32[]{:S(2)}, u32[]{:S(2)}) %collective-permute-start.1) | collective-permute-done | bytes 1048608 | tf_op jit(solution)/shard_map/ppermute | solution.py:16
  82.6 3.4 collective-permute-start.2
  85.9 31.1 %collective-permute-done.2 = bf16[512,2048]{1,0:T(8,128)(2,1)S(1)} collective-permute-done((bf16[512,2048]{1,0:T(8,128)(2,1)S(1)}, bf16[512,2048]{1,0:T(8,128)(2,1)S(1)}, u32[]{:S(2)}, u32[]{:S(2)}) %collective-permute-start.2) | collective-permute-done | bytes 2097184 | tf_op jit(solution)/shard_map/ppermute | solution.py:16
  117.0 3.6 pad_maximum_fusion
  129.1 4.7 fusion.77
  133.9 80.5 %collective-permute-done.3 = bf16[1024,2048]{1,0:T(8,128)(2,1)} collective-permute-done((bf16[1024,2048]{1,0:T(8,128)(2,1)}, bf16[1024,2048]{1,0:T(8,128)(2,1)}, u32[]{:S(2)}, u32[]{:S(2)}) %collective-permute-start.3) | collective-permute-done | bytes 4194336 | tf_op jit(solution)/shard_map/ppermute | solution.py:16
  214.3 6.8 constant_dynamic-update-slice_fusion
  225.2 45.1 %all-gather.7.cloned.1.call-done = bf16[4096,512]{1,0:T(8,128)(2,1)} async-done(((bf16[128,512]{1,0:T(8,128)(2,1)}), bf16[4096,512]{1,0:T(8,128)(2,1)}) %all-gather.7.cloned.1.call-update) | async-done | bytes 4194320 | tf_op jit(solution)/shard_map/all_gather | solution.py:75
  270.4 4.7 fusion.80
  275.1 10.7 %fusion.71 = bf16[1024,512]{0,1:T(8,128)(2,1)} fusion(bf16[4096,512]{1,0:T(8,128)(2,1)} %all-gather.5.cloned.1.call-done, bf16[1,1024,4096]{2,1,0:T(8,128)(2,1)} %param.9), kind=kOutput, calls=%fused_computation.75 | convolution fusion | flops 4295491584 | bytes 13631488 | tf_op jit(solution)/shard_map/dot_general | solution.py:78
  285.8 8.4 %fusion.74 = bf16[1024,512]{0,1:T(8,128)(2,1)} fusion(bf16[4096,512]{1,0:T(8,128)(2,1)S(1)} %copy-done.12, bf16[1,1024,4096]{2,1,0:T(8,128)(2,1)} %param.9), kind=kOutput, calls=%fused_computation.76 | convolution fusion | flops 4295491584 | bytes 13631488 | tf_op jit(solution)/shard_map/dot_general | solution.py:78
  294.3 144.1 %collective-permute-done.4 = bf16[2048,2048]{1,0:T(8,128)(2,1)} collective-permute-done((bf16[2048,2048]{1,0:T(8,128)(2,1)}, bf16[2048,2048]{1,0:T(8,128)(2,1)}, u32[]{:S(2)}, u32[]{:S(2)}) %collective-permute-start.4) | collective-permute-done | bytes 8388640 | tf_op jit(solution)/shard_map/ppermute | solution.py:16
  438.3 8.4 %constant_dynamic-update-slice_fusion.11 = bf16[8192,2048]{1,0:T(8,128)(2,1)} fusion(bf16[8192,2048]{1,0:T(8,128)(2,1)} %get-tuple-element.142, bf16[2048,2048]{1,0:T(8,128)(2,1)} %collective-permute-done.4), kind=kLoop, calls=%fused_computation.91 | loop fusion | bytes 16777216
  453.0 4.8 constant_dynamic-update-slice_fusion.6
  457.8 8.3 %constant_dynamic-update-slice_fusion.5 = bf16[8192,2048]{1,0:T(8,128)(2,1)} fusion(bf16[8192,2048]{1,0:T(8,128)(2,1)} %constant_dynamic-update-slice_fusion.6, bf16[2048,2048]{1,0:T(8,128)(2,1)} %collective-permute-done.4), kind=kLoop, calls=%fused_computation.85 | loop fusion | bytes 16777216 | tf_op jit(solution)/shard_map/jit(_roll_dynamic)/concatenate | solution.py:20
  466.1 13.3 %fusion.60 = bf16[384,2048]{0,1:T(8,128)(2,1)} fusion(bf16[1,384,4096]{2,1,0:T(8,128)(2,1)S(1)} %copy-done, bf16[8192,2048]{1,0:T(8,128)(2,1)} %constant_dynamic-update-slice_fusion.5, s32[]{:T(128)S(6)} %select_n.45), kind=kOutput, calls=%fused_computation.69 | convolution fusion | flops 6443237376 | bytes 21495812 | tf_op jit(solution)/shard_map/dot_general | solution.py:81
  482.3 24.1 %convert_bitcast_fusion = bf16[1024,2048]{0,1:T(8,128)(2,1)} fusion(bf16[1,1024,4096]{2,1,0:T(8,128)(2,1)} %param.9, bf16[8192,2048]{1,0:T(8,128)(2,1)} %constant_dynamic-update-slice_fusion.5, s32[]{:T(128)S(6)} %select_n.45), kind=kOutput, calls=%fused_computation.60 | convolution fusion | flops 17181966336 | bytes 29360132 | tf_op jit(solution)/shard_map/dot_general | solution.py:78
  506.4 167.2 %while.16 = (s32[]{:T(128)}, f32[4,4,384]{2,1,0:T(4,128)S(1)}, f32[4,4,384]{2,1,0:T(4,128)S(1)}, f32[4,4,384,128]{3,2,1,0:T(8,128)}, s32[6]{0:T(128)S(1)}, /*ind...) while((s32[]{:T(128)}, f32[4,4,384]{2,1,0:T(4,128)S(1)}, ...), condition=%wide.wide.region_7.8_spmd.clone, body=%wide.wide.region_4.7_spmd.clone.sunk | while | flops 1654292352 | bytes 52043940 | solution.py:128
  512.7 6.0 fusion.128
  518.7 6.5 fusion.129
  525.4 8.5 %fusion.131 = f32[4,4,384,128]{3,2,1,0:T(8,128)} fusion(f32[4,4,384,128]{3,2,1,0:T(8,128)} %get-tuple-element.304, bf16[512,4,128,1]{0,2,3,1:T(8,128)(2,1)S(1)} %bitcast.155, f32[4,512,384,4]{2,1,3,0:T(8,128)} %get-tuple-element.284, f32[4,4,384]{2,1,0:T(4,128)S(1)} %select_maximum_fusion.3, pred[384,512]{0,1:T(8,128)(4,1)S(1)} %compare_and_fusion.3, ...), kind=kOutput, calls=%fused_computation.9.clone.clone.1 | convolution fusion | flops 823394304 | bytes 19644416 | tf_op jit(solution)/shard_map/while/body/eval_jaxpr/hgbk,khd->hgbd/dot_general | solution.py:34
  540.2 6.0 fusion.128
  546.2 6.5 fusion.129
  552.9 8.9 %fusion.131 = f32[4,4,384,128]{3,2,1,0:T(8,128)} fusion(f32[4,4,384,128]{3,2,1,0:T(8,128)} %get-tuple-element.304, bf16[512,4,128,1]{0,2,3,1:T(8,128)(2,1)S(1)} %bitcast.155, f32[4,512,384,4]{2,1,3,0:T(8,128)} %get-tuple-element.284, f32[4,4,384]{2,1,0:T(4,128)S(1)} %select_maximum_fusion.3, pred[384,512]{0,1:T(8,128)(4,1)S(1)} %compare_and_fusion.3, ...), kind=kOutput, calls=%fused_computation.9.clone.clone.1 | convolution fusion | flops 823394304 | bytes 19644416 | tf_op jit(solution)/shard_map/while/body/eval_jaxpr/hgbk,khd->hgbd/dot_general | solution.py:34
  568.1 6.0 fusion.128
  574.1 6.5 fusion.129
  580.9 8.9 %fusion.131 = f32[4,4,384,128]{3,2,1,0:T(8,128)} fusion(f32[4,4,384,128]{3,2,1,0:T(8,128)} %get-tuple-element.304, bf16[512,4,128,1]{0,2,3,1:T(8,128)(2,1)S(1)} %bitcast.155, f32[4,512,384,4]{2,1,3,0:T(8,128)} %get-tuple-element.284, f32[4,4,384]{2,1,0:T(4,128)S(1)} %select_maximum_fusion.3, pred[384,512]{0,1:T(8,128)(4,1)S(1)} %compare_and_fusion.3, ...), kind=kOutput, calls=%fused_computation.9.clone.clone.1 | convolution fusion | flops 823394304 | bytes 19644416 | tf_op jit(solution)/shard_map/while/body/eval_jaxpr/hgbk,khd->hgbd/dot_general | solution.py:34
  596.1 6.0 fusion.128
  602.1 6.5 fusion.129
  608.8 8.9 %fusion.131 = f32[4,4,384,128]{3,2,1,0:T(8,128)} fusion(f32[4,4,384,128]{3,2,1,0:T(8,128)} %get-tuple-element.304, bf16[512,4,128,1]{0,2,3,1:T(8,128)(2,1)S(1)} %bitcast.155, f32[4,512,384,4]{2,1,3,0:T(8,128)} %get-tuple-element.284, f32[4,4,384]{2,1,0:T(4,128)S(1)} %select_maximum_fusion.3, pred[384,512]{0,1:T(8,128)(4,1)S(1)} %compare_and_fusion.3, ...), kind=kOutput, calls=%fused_computation.9.clone.clone.1 | convolution fusion | flops 823394304 | bytes 19644416 | tf_op jit(solution)/shard_map/while/body/eval_jaxpr/hgbk,khd->hgbd/dot_general | solution.py:34
  624.0 6.0 fusion.128
  630.0 6.5 fusion.129
  636.7 8.9 %fusion.131 = f32[4,4,384,128]{3,2,1,0:T(8,128)} fusion(f32[4,4,384,128]{3,2,1,0:T(8,128)} %get-tuple-element.304, bf16[512,4,128,1]{0,2,3,1:T(8,128)(2,1)S(1)} %bitcast.155, f32[4,512,384,4]{2,1,3,0:T(8,128)} %get-tuple-element.284, f32[4,4,384]{2,1,0:T(4,128)S(1)} %select_maximum_fusion.3, pred[384,512]{0,1:T(8,128)(4,1)S(1)} %compare_and_fusion.3, ...), kind=kOutput, calls=%fused_computation.9.clone.clone.1 | convolution fusion | flops 823394304 | bytes 19644416 | tf_op jit(solution)/shard_map/while/body/eval_jaxpr/hgbk,khd->hgbd/dot_general | solution.py:34
  651.9 6.0 fusion.128
  657.9 6.5 fusion.129
  664.7 8.9 %fusion.131 = f32[4,4,384,128]{3,2,1,0:T(8,128)} fusion(f32[4,4,384,128]{3,2,1,0:T(8,128)} %get-tuple-element.304, bf16[512,4,128,1]{0,2,3,1:T(8,128)(2,1)S(1)} %bitcast.155, f32[4,512,384,4]{2,1,3,0:T(8,128)} %get-tuple-element.284, f32[4,4,384]{2,1,0:T(4,128)S(1)} %select_maximum_fusion.3, pred[384,512]{0,1:T(8,128)(4,1)S(1)} %compare_and_fusion.3, ...), kind=kOutput, calls=%fused_computation.9.clone.clone.1 | convolution fusion | flops 823394304 | bytes 19644416 | tf_op jit(solution)/shard_map/while/body/eval_jaxpr/hgbk,khd->hgbd/dot_general | solution.py:34
  673.6 2.8 divide_bitcast_fusion
  680.0 3.8 fusion.89
  683.8 20.4 %fusion.92 = (f32[4,4,512]{2,1,0:T(4,128)S(1)}, bf16[4,4,512,1024]{2,3,1,0:T(8,128)(2,1)}) fusion(bf16[1024,4,128,1]{0,2,3,1:T(8,128)(2,1)} %bitcast.167, bf16[512,4,4,128]{0,3,2,1:T(8,128)(2,1)S(1)} %bitcast.161, pred[512,1024]{0,1:T(8,128)(4,1)S(1)} %copy-done.9), kind=kOutput, calls=%fused_computation.108 | convolution fusion | flops 2197816320 | bytes 20480000 | tf_op jit(solution)/shard_map/sub | solution.py:55
  704.3 8.5 %fusion.45 = bf16[512,4,4,128]{0,3,2,1:T(8,128)(2,1)S(1)} fusion(bf16[1024,4,128,1]{0,2,3,1:T(8,128)(2,1)} %bitcast.165, bf16[4,4,512,1024]{2,3,1,0:T(8,128)(2,1)} %get-tuple-element.158, f32[512,4,4]{0,2,1:T(4,128)S(1)} %bitcast.170), kind=kOutput, calls=%fused_computation.59 | convolution fusion | flops 2149580800 | bytes 19955712 | tf_op jit(solution)/shard_map/hgbk,khd->hgbd/dot_general | solution.py:34
  712.8 2.5 copy.31
  715.3 20.8 %fusion.91 = (f32[4,4,512]{2,1,0:T(4,128)S(1)}, bf16[4,4,512,1024]{2,3,1,0:T(8,128)(2,1)}) fusion(bf16[1024,4,128,1]{0,2,3,1:T(8,128)(2,1)} %bitcast.168, bf16[512,4,4,128]{0,3,2,1:T(8,128)(2,1)} %bitcast.160, pred[512,1024]{0,1:T(8,128)(4,1)S(1)} %copy-done.8), kind=kOutput, calls=%fused_computation.107 | convolution fusion | flops 2197816320 | bytes 20480000 | tf_op jit(solution)/shard_map/sub | solution.py:55
  736.1 9.9 %fusion.44 = bf16[512,4,4,128]{0,3,2,1:T(8,128)(2,1)} fusion(bf16[1024,4,128,1]{0,2,3,1:T(8,128)(2,1)} %bitcast.166, bf16[4,4,512,1024]{2,3,1,0:T(8,128)(2,1)} %get-tuple-element.156, f32[512,4,4]{0,2,1:T(4,128)S(1)} %bitcast.169), kind=kOutput, calls=%fused_computation.57 | convolution fusion | flops 2149580800 | bytes 19955712 | tf_op jit(solution)/shard_map/hgbk,khd->hgbd/dot_general | solution.py:34
  746.1 4.0 copy.32
  750.0 2.9 select_convert_fusion
  752.9 4.8 pad_maximum_fusion.1
  (131 shorter events, 67.8 us)
Async XLA Ops:
  7.2 121.9 %copy-start = (bf16[1,384,4096]{2,1,0:T(8,128)(2,1)S(1)}, bf16[1,384,4096]{2,1,0:T(8,128)(2,1)}, u32[]{:S(2)}) copy-start(bf16[1,384,4096]{2,1,0:T(8,128)(2,1)} %param.11) | copy-start | bytes 9437188
  7.2 121.9 %all-gather.5.cloned.1.call-start = ((), (), s32[]{:S(2)}) async-start(), calls=%async_computation | async-start | bytes 4325376 | tf_op jit(solution)/shard_map/all_gather | solution.py:74
  7.9 262.5 %all-gather.7.cloned.1.call-start = ((), (), s32[]{:S(2)}) async-start(), calls=%async_computation.1 | async-start | bytes 4325376 | tf_op jit(solution)/shard_map/all_gather | solution.py:75
  8.0 18.2 %collective-permute-start = (bf16[128,2048]{1,0:T(8,128)(2,1)}, bf16[128,2048]{1,0:T(8,128)(2,1)}, u32[]{:S(2)}, u32[]{:S(2)}) collective-permute-start(bf16[128,2048]{1,0:T(8,128)(2,1)} %param.13), channel_id=1, source_target_pairs={{0,31},{1,0},{2,1},{3,2},{4,3},{5,4},{6,5},{7,6},{8,7},{9,8},{10,9... | collective-permute-start | bytes 1572872 | tf_op jit(solution)/shard_map/ppermute | solution.py:16
  14.4 492.0 %all-gather.9.cloned.1.call-start = ((), (), s32[]{:S(2)}) async-start(), calls=%async_computation.2 | async-start | bytes 3538944 | tf_op jit(solution)/shard_map/all_gather | solution.py:100
  14.5 107.2 %copy-start.6 = (bf16[128,2048]{1,0:T(8,128)(2,1)S(1)}, bf16[128,2048]{1,0:T(8,128)(2,1)}, u32[]{:S(2)}) copy-start(bf16[128,2048]{1,0:T(8,128)(2,1)} %param.13) | copy-start | bytes 1572868
  27.4 53.4 %collective-permute-start.1 = (bf16[256,2048]{1,0:T(8,128)(2,1)S(1)}, bf16[256,2048]{1,0:T(8,128)(2,1)S(1)}, u32[]{:S(2)}, u32[]{:S(2)}) collective-permute-start(bf16[256,2048]{1,0:T(8,128)(2,1)S(1)} %pad_maximum_fusion.3), channel_id=1, source_target_pairs={{0,30},{1,31},{2,0},{3,1},{4,2},{5,3},{6,4},{7,5},{8,6},{9,7},{10,... | collective-permute-start | bytes 3145736 | tf_op jit(solution)/shard_map/ppermute | solution.py:16
  80.8 45.8 %copy-start.4 = (bf16[256,2048]{1,0:T(8,128)(2,1)}, bf16[256,2048]{1,0:T(8,128)(2,1)S(1)}, u32[]{:S(2)}) copy-start(bf16[256,2048]{1,0:T(8,128)(2,1)S(1)} %collective-permute-done.1) | copy-start | bytes 3145732
  82.6 34.5 %collective-permute-start.2 = (bf16[512,2048]{1,0:T(8,128)(2,1)S(1)}, bf16[512,2048]{1,0:T(8,128)(2,1)S(1)}, u32[]{:S(2)}, u32[]{:S(2)}) collective-permute-start(bf16[512,2048]{1,0:T(8,128)(2,1)S(1)} %pad_maximum_fusion.2), channel_id=1, source_target_pairs={{0,28},{1,29},{2,30},{3,31},{4,0},{5,1},{6,2},{7,3},{8,4},{9,5},{1... | collective-permute-start | bytes 6291464 | tf_op jit(solution)/shard_map/ppermute | solution.py:16
  117.0 9.5 %copy-start.2 = (bf16[512,2048]{1,0:T(8,128)(2,1)}, bf16[512,2048]{1,0:T(8,128)(2,1)S(1)}, u32[]{:S(2)}) copy-start(bf16[512,2048]{1,0:T(8,128)(2,1)S(1)} %collective-permute-done.2) | copy-start | bytes 6291460
  120.7 93.6 %collective-permute-start.3 = (bf16[1024,2048]{1,0:T(8,128)(2,1)}, bf16[1024,2048]{1,0:T(8,128)(2,1)}, u32[]{:S(2)}, u32[]{:S(2)}) collective-permute-start(bf16[1024,2048]{1,0:T(8,128)(2,1)} %pad_maximum_fusion), channel_id=1, source_target_pairs={{0,24},{1,25},{2,26},{3,27},{4,28},{5,29},{6,30},{7,31},{8,0},{9,1... | collective-permute-start | bytes 12582920 | tf_op jit(solution)/shard_map/ppermute | solution.py:16
  133.8 89.5 %copy-start.10 = (s32[1,1024]{1,0:T(1,128)S(1)}, s32[1,1024]{1,0:T(1,128)}, u32[]{:S(2)}) copy-start(s32[1,1024]{1,0:T(1,128)} %param.10) | copy-start | bytes 12292
  133.8 372.6 %all-gather.11.cloned.1.call-start = ((), (), s32[]{:S(2)}) async-start(), calls=%async_computation.3 | async-start | bytes 3538944 | tf_op jit(solution)/shard_map/all_gather | solution.py:101
  221.1 217.2 %collective-permute-start.4 = (bf16[2048,2048]{1,0:T(8,128)(2,1)}, bf16[2048,2048]{1,0:T(8,128)(2,1)}, u32[]{:S(2)}, u32[]{:S(2)}) collective-permute-start(bf16[2048,2048]{1,0:T(8,128)(2,1)} %get-tuple-element.141), channel_id=1, source_target_pairs={{0,16},{1,17},{2,18},{3,19},{4,20},{5,21},{6,22},{7,23},{8,24},{9,... | collective-permute-start | bytes 25165832 | tf_op jit(solution)/shard_map/ppermute | solution.py:16
  275.1 10.7 %copy-start.12 = (bf16[4096,512]{1,0:T(8,128)(2,1)S(1)}, bf16[4096,512]{1,0:T(8,128)(2,1)}, u32[]{:S(2)}) copy-start(bf16[4096,512]{1,0:T(8,128)(2,1)} %all-gather.7.cloned.1.call-done) | copy-start | bytes 12582916
  438.3 12.2 %copy-start.5 = (bf16[256,2048]{1,0:T(8,128)(2,1)S(1)}, bf16[256,2048]{1,0:T(8,128)(2,1)}, u32[]{:S(2)}) copy-start(bf16[256,2048]{1,0:T(8,128)(2,1)} %copy-done.4) | copy-start | bytes 3145732
  438.3 13.2 %copy-start.3 = (bf16[512,2048]{1,0:T(8,128)(2,1)S(1)}, bf16[512,2048]{1,0:T(8,128)(2,1)}, u32[]{:S(2)}) copy-start(bf16[512,2048]{1,0:T(8,128)(2,1)} %copy-done.2) | copy-start | bytes 6291460
  481.2 25.3 %copy-start.7 = (bf16[384,2048]{1,0:T(8,128)(2,1)}, bf16[384,2048]{1,0:T(8,128)(2,1)S(1)}, u32[]{:S(2)}) copy-start(bf16[384,2048]{1,0:T(8,128)(2,1)S(1)} %copy.34) | copy-start | bytes 4718596
  677.6 6.2 copy-start.9
  704.3 11.0 %copy-start.8 = (pred[512,1024]{0,1:T(8,128)(4,1)S(1)}, pred[512,1024]{0,1:T(8,128)(4,1)}, u32[]{:S(2)}) copy-start(pred[512,1024]{0,1:T(8,128)(4,1)} %get-tuple-element.152) | copy-start | bytes 1572868
  736.1 13.9 %copy-start.11 = (pred[384]{0:T(512)(128)(4,1)S(1)}, pred[384]{0:T(512)(128)(4,1)}, u32[]{:S(2)}) copy-start(pred[384]{0:T(512)(128)(4,1)} %add_compare_fusion) | copy-start | bytes 1156
  736.1 21.6 %copy-start.1 = (bf16[1,384,4096]{2,1,0:T(8,128)(2,1)S(1)}, bf16[1,384,4096]{2,1,0:T(8,128)(2,1)}, u32[]{:S(2)}) copy-start(bf16[1,384,4096]{2,1,0:T(8,128)(2,1)} %param.11) | copy-start | bytes 9437188
Sparse Core Ops, SparseCore 0:
  11.0 98.6 all-gather.4
  112.7 157.6 all-gather.6
  272.3 43.8 all-gather.8
  317.9 45.0 all-gather.10
